TPU v7x, 32 devices: a whole 2x2x4 slice. The times are simulated.
32 devices in a mesh: dp: 2 (over x), cp: 4 (over z), tp: 4 (over y, core).
Axes of the slice: x: 2, y: 2, z: 4, core: 2. Of those that a mesh axis runs over, the one named last changes fastest.
Arguments:
- x: bfloat16 [8192, 2048], P(('dp', 'cp', 'tp')), parts along dimension 0
- idx: int32 [8192, 2], P(('dp', 'cp', 'tp')), parts along dimension 0
- gates: float32 [8192, 2], P(('dp', 'cp', 'tp')), parts along dimension 0
- wq: bfloat16 [2048, 2048], P(None, 'tp')
- wk: bfloat16 [2048, 2048], P(None, 'tp')
- wv: bfloat16 [2048, 2048], P(None, 'tp')
- wo: bfloat16 [2048, 2048], P('tp')
- w1g: bfloat16 [16, 2048, 1024], P(('cp', 'tp'))
- w1u: bfloat16 [16, 2048, 1024], P(('cp', 'tp'))
- w2: bfloat16 [16, 1024, 2048], P(('cp', 'tp'))
Outputs:
- output: bfloat16 [8192, 2048], P(('dp', 'cp', 'tp')), parts along dimension 0
There are 2 independent parts. A program takes and returns all parts, laid end to end along the dimension named above; an argument that names none is the same for every part.
All inputs are finite; a program needn't handle non-finite values.
Results may differ from a plain program's by a relative error of at most 0.00999393.
Values are sent between devices in bfloat16 or wider.
A program may use at most 1 GiB of HBM per device.

v0:
```python
import functools

import jax
import jax.numpy as jnp
from jax import lax
from jax.experimental import pallas as pl
from jax.experimental.pallas import tpu as pltpu
from jax.sharding import PartitionSpec as P

HD = 128
BF = jnp.bfloat16
F32 = jnp.float32
MESH = pl.DeviceIdType.MESH
NEG = -1e30
ANY = pl.BlockSpec(memory_space=pl.ANY)
VM = pl.BlockSpec(memory_space=pltpu.VMEM)
MIB = 2 ** 20
BASE_CAP, FULL_CAP = 32, 64
ORDER = (4, 5, 6, 7, 8, 9, 10, 11, 12, 13, 14, 15, 1, 2, 3, 0)


def remote(src, dst, ssem, rsem, c, t):
    return pltpu.make_async_remote_copy(
        src_ref=src, dst_ref=dst, send_sem=ssem, recv_sem=rsem,
        device_id={'cp': c, 'tp': t}, device_id_type=MESH)


def group_barrier(c, t):
    sem = pltpu.get_barrier_semaphore()
    for i in range(1, 16):
        pl.semaphore_signal(sem, inc=1, device_id={'cp': c ^ (i // 4), 'tp': t ^ (i % 4)}, device_id_type=MESH)
    pl.semaphore_wait(sem, 15)


def kernel_ab(x_ref, it_ref, gt_ref, wq_ref, wk_ref, wv_ref, wo_ref, w1g_ref, w1u_ref, w2_ref,
              y_ref, h_out, over_ref,
              xs, wq, wk, wv, sqk, sv, qk, vt, acc, mx, ls, wob, ob, orecv, hs, cb, cnt,
              wg, wu, wd, sb, rb, zb, bb,
              ldsem, xsend, xrecv, wsend, wrecv, bsend, brecv, bloc, osend, orsem, csend, crecv, hsem, esem, *csems):
    c = lax.axis_index('cp')
    t = lax.axis_index('tp')
    y = t // 2
    odd = lax.rem(t, 2) == 1
    rows = it_ref.shape[1]
    seg = 2 * rows
    nseg = 8
    me = c * 4 + t

    def has(cc, sl, s):
        outer = jnp.logical_or(s < 2, s > 5)
        kvg = jnp.where(cc < 2, outer, jnp.logical_not(outer))
        moved = jnp.where(cc < 2, s < 2, s >= 2)
        return jnp.where(jnp.logical_and(odd, sl == 1), moved, kvg)

    def sees(cc, sl, s):
        moved = jnp.where(cc < 2, 1, 7)
        return s <= jnp.where(jnp.logical_and(odd, sl == 1), moved, jnp.where(cc < 2, 7, 5))

    own = pl.ds(pl.multiple_of(t * rows, rows), rows)
    loads = [pltpu.make_async_copy(a, b, ldsem.at[i])
             for i, (a, b) in enumerate(((x_ref, xs.at[own]), (wk_ref, wk), (wv_ref, wv), (wq_ref, wq), (wo_ref, wob.at[t])))]
    for cp in loads:
        cp.start()
    e = lax.broadcasted_iota(jnp.int32, (HD, rows), 0)
    hit = (it_ref[0:1, :] == e).astype(F32) + (it_ref[1:2, :] == e).astype(F32)
    load = jnp.max(jnp.sum(hit, axis=1, keepdims=True), axis=0, keepdims=True)
    cb[...] = jnp.broadcast_to(load, cb.shape)
    cnt[me] = cb[...]
    group_barrier(c, t)
    pending = []

    def go(cp):
        cp.start()
        pending.append(cp)

    loads[0].wait()
    go(remote(xs.at[own], xs.at[own], xsend.at[0], xrecv.at[t], c, t ^ 1))
    go(remote(xs.at[own], xs.at[own], xsend.at[1], xrecv.at[t], c, t ^ 2))

    def xwait(tt):
        r = pl.ds(pl.multiple_of(tt * rows, rows), rows)
        remote(xs.at[r], xs.at[r], xsend.at[0], xrecv.at[tt], c, t ^ 1).wait_recv()

    def blocks(m, p, cc, sl, s):
        hd = 2 * sl + lax.rem(cc, 2)
        if m == 2:
            return sv.at[p, hd], vt.at[sl, s]
        return sqk.at[p, m, hd], qk.at[sl, m, s]

    def need(m, cc, sl, s):
        return has(cc, sl, s) if m == 0 else sees(cc, sl, s)

    def block_copy(m, p, off, sl, s):
        cc = c ^ off
        src, dst = blocks(m, p, cc, sl, s)
        return need(m, cc, sl, s), remote(src, dst, bsend.at[p, m, off, sl], brecv.at[sl, m, s], cc, t)

    def own_copy(m, p, sl, s):
        src, dst = blocks(m, p, c, sl, s)
        return need(m, c, sl, s), pltpu.make_async_copy(src, dst, bloc.at[p, m, sl])

    def half(p, row0, s):
        for sl in range(2):
            wide = slice(2 * sl * HD, 2 * (sl + 1) * HD)
            for m, w, ld in ((1, wk, 1), (2, wv, 2), (0, wq, 3)):
                if p == 0 and sl == 0:
                    loads[ld].wait()
                r = jnp.dot(xs[pl.ds(row0, seg), :], w[:, wide], preferred_element_type=F32)
                if m == 2:
                    rt = r.T.astype(BF)
                    for hh in range(2):
                        sv[p, 2 * sl + hh] = rt[hh * HD:(hh + 1) * HD]
                else:
                    r = r.astype(BF)
                    for hh in range(2):
                        sqk[p, m, 2 * sl + hh] = r[:, hh * HD:(hh + 1) * HD]
                for off in (1, 2, 3):
                    ok, cp = block_copy(m, p, off, sl, s)
                    pl.when(ok)(cp.start)
                ok, cp = own_copy(m, p, sl, s)
                pl.when(ok)(cp.start)

    seg0 = jnp.where(y == 0, c, nseg - 1 - c)
    seg1 = jnp.where(y == 0, nseg - 1 - c, c)
    xwait(t ^ 1)
    half(0, pl.multiple_of(y * seg, seg), seg0)
    loads[4].wait()
    go(remote(wob.at[t], wob.at[t], wsend.at[0], wrecv.at[t], c, t ^ 1))
    go(remote(wob.at[t], wob.at[t], wsend.at[1], wrecv.at[t], c, t ^ 2))
    for i in range(1, 16):
        go(remote(cb, cnt.at[me], csend.at[i], crecv.at[me], c ^ (i // 4), t ^ (i % 4)))
    acc[...] = jnp.zeros_like(acc)
    mx[...] = jnp.full_like(mx, NEG)
    ls[...] = jnp.zeros_like(ls)
    xwait(t ^ 2)
    r2 = pl.ds(pl.multiple_of((t ^ 2) * rows, rows), rows)
    go(remote(xs.at[r2], xs.at[r2], xsend.at[2], xrecv.at[t ^ 2], c, t ^ 1))
    xwait(t ^ 3)
    half(1, pl.multiple_of((1 - y) * seg, seg), seg1)
    wl = expert_loads(w1g_ref, w1u_ref, w2_ref, wg, wu, wd, esem)
    for cp in wl:
        cp.start()

    k2 = (HD ** -0.5) * 1.4426950408889634

    def unit(sl, q, j, diag):
        sc = lax.dot_general(qk[sl, 1, j], qk[sl, 0, q], (((1,), (1,)), ((), ())), preferred_element_type=F32)
        if diag:
            ki = lax.broadcasted_iota(jnp.int32, sc.shape, 0)
            qi = lax.broadcasted_iota(jnp.int32, sc.shape, 1)
            sc = jnp.where(ki <= qi, sc, NEG)
        m = mx[sl, q]
        mn = jnp.maximum(m, jnp.max(sc, axis=0, keepdims=True))
        w = jnp.exp2((sc - mn) * k2)
        a = jnp.exp2((m - mn) * k2)
        mx[sl, q] = mn
        ls[sl, q] = ls[sl, q] * a + jnp.sum(w, axis=0, keepdims=True)
        acc[sl, q] = acc[sl, q] * a + jnp.dot(vt[sl, j], w.astype(BF), preferred_element_type=F32)

    inner = jnp.logical_or(c == 1, c == 2)

    def off_of(i):
        r = lax.rem(i, 4)
        far = jnp.where(inner, 5 - r, r)
        return jnp.where(r < 2, r, far)

    def seg_of(i):
        cc = c ^ off_of(i)
        low = (i < 4) == (y == 0)
        return jnp.where(low, cc, nseg - 1 - cc)

    def pos_of(s):
        low = s < 4
        off = jnp.where(low, s, nseg - 1 - s) ^ c
        far = jnp.where(inner, 5 - off, off)
        return jnp.where(low == (y == 0), 0, 4) + jnp.where(off < 2, off, far)

    def dest(s, hf):
        low = s < 4
        return jnp.where(low, s, nseg - 1 - s), jnp.where(low, hf, 2 + hf)

    def ocopy(sl, s, hf):
        c2, t2 = dest(s, hf)
        hd = t * 4 + 2 * sl + lax.rem(c, 2)
        src = ob.at[sl, s, pl.ds(hf * rows, rows)]
        dst = orecv.at[:, pl.ds(pl.multiple_of(hd * HD, HD), HD)]
        rm = remote(src, dst, osend.at[sl, s, hf], orsem.at[hd], c2, t2)
        lc = pltpu.make_async_copy(src, dst, orsem.at[hd])
        return jnp.logical_and(c2 == c, t2 == t), rm, lc

    def finish(sl, s):
        ob[sl, s] = (acc[sl, s] * (1.0 / ls[sl, s])).T.astype(BF)
        for hf in range(2):
            mine, rm, lc = ocopy(sl, s, hf)
            pl.when(jnp.logical_not(mine))(rm.start)
            pl.when(mine)(lc.start)

    def event(ev, _):
        p = ev // 8
        sl = lax.rem(ev // 4, 2)
        i = p * 4 + lax.rem(ev, 4)
        s = seg_of(i)
        off = off_of(i)
        for m in range(3):
            src, dst = blocks(m, p, c, sl, s)
            ok = need(m, c, sl, s)
            pl.when(jnp.logical_and(ok, off != 0))(
                remote(src, dst, bsend.at[0, 0, 0, 0], brecv.at[sl, m, s], c, t ^ 1).wait_recv)
            pl.when(jnp.logical_and(ok, off == 0))(
                pltpu.make_async_copy(src, dst, bloc.at[p, m, sl]).wait)

        def pair(k, _):
            s2 = seg_of(k)
            q, j = jnp.maximum(s, s2), jnp.minimum(s, s2)

            @pl.when(has(c, sl, q))
            def _():
                unit(sl, q, j, False)
            return 0

        lax.fori_loop(0, i, pair, 0)

        @pl.when(has(c, sl, s))
        def _():
            unit(sl, s, s, True)

        def done(q, last):
            last = jnp.maximum(last, pos_of(q))

            @pl.when(jnp.logical_and(last == i, has(c, sl, q)))
            def _():
                finish(sl, q)
            return last

        lax.fori_loop(0, nseg, done, 0)
        return 0

    lax.fori_loop(0, 16, event, 0)

    def wwait(tt):
        remote(wob.at[t], wob.at[tt], wsend.at[0], wrecv.at[tt], c, t ^ 1).wait_recv()

    wwait(t ^ 2)
    go(remote(wob.at[t ^ 2], wob.at[t ^ 2], wsend.at[2], wrecv.at[t ^ 2], c, t ^ 1))
    for i in range(1, 16):
        other = (c ^ (i // 4)) * 4 + (t ^ (i % 4))
        remote(cb, cnt.at[other], csend.at[i], crecv.at[other], c ^ (i // 4), t ^ (i % 4)).wait_recv()
    worst = jnp.max(cnt[...])
    over_ref[0] = (worst > BASE_CAP).astype(jnp.int32)
    for tt in range(4):
        for hd in range(4):
            k = tt * 4 + hd
            half_b = jnp.logical_and(seg0 >= 2, seg0 <= 5)
            if hd >= 2 and tt % 2 == 1:
                half_b = seg0 >= 2
            cp_ = jnp.where(half_b, 2, 0) + hd % 2
            mine = jnp.logical_and(cp_ == c, t == tt)
            dst = orecv.at[:, k * HD:(k + 1) * HD]
            src = ob.at[0, 0, pl.ds(0, rows)]
            pl.when(jnp.logical_not(mine))(remote(src, dst, osend.at[0, 0, 0], orsem.at[k], c, t ^ 1).wait_recv)
            pl.when(mine)(pltpu.make_async_copy(src, dst, orsem.at[k]).wait)
    wwait(t ^ 1)
    wwait(t ^ 3)
    for nb in range(4):
        cols = slice(nb * 512, (nb + 1) * 512)
        a = xs[own, cols].astype(F32)
        p = jnp.zeros_like(a)
        for tt in range(4):
            p = p + jnp.dot(orecv[:, tt * 512:(tt + 1) * 512], wob[tt, :, cols], preferred_element_type=F32)
        hs[:, cols] = (a + p).astype(BF)
    hcp = pltpu.make_async_copy(hs, h_out, hsem.at[0])
    hcp.start()
    experts(BASE_CAP, c, t, hs, it_ref[...], gt_ref[...], y_ref, wl, wg, wu, wd, sb, rb, zb, bb, *csems)
    hcp.wait()
    for cp in pending:
        cp.wait_send()
    for p, s in ((0, seg0), (1, seg1)):
        for m in range(3):
            for off in (1, 2, 3):
                for sl in range(2):
                    ok, cp = block_copy(m, p, off, sl, s)
                    pl.when(ok)(cp.wait_send)

    def drain(s, _):
        for sl in range(2):
            for hf in range(2):
                mine, rm, lc = ocopy(sl, s, hf)
                pl.when(jnp.logical_and(has(c, sl, s), jnp.logical_not(mine)))(rm.wait_send)
        return 0

    lax.fori_loop(0, nseg, drain, 0)


def experts(cap, c, t, h_ref, it, gt, y_ref, wl, wg, wu, wd, sb, rb, zb, bb, dsend, drecv, zsend, zrecv, dloc, zloc):
    me = c * 4 + t
    rows = h_ref.shape[0]
    ne = 16
    ei = lax.broadcasted_iota(jnp.int32, (HD, rows), 0)
    o0 = (it[0:1, :] == ei).astype(F32)
    o1 = (it[1:2, :] == ei).astype(F32)
    ri = lax.broadcasted_iota(jnp.int32, (rows, rows), 0)
    ci = lax.broadcasted_iota(jnp.int32, (rows, rows), 1)
    rank = jnp.dot((o0 + o1).astype(BF), (ri < ci).astype(BF), preferred_element_type=F32)
    base = jnp.where(rank < cap, ei.astype(F32) * cap + rank, -1.0)
    d0 = jnp.sum(o0 * base, axis=0, keepdims=True)
    d1 = jnp.sum(o1 * base, axis=0, keepdims=True)
    ki = lax.broadcasted_iota(jnp.int32, (ne * cap, rows), 0).astype(F32)
    pack = jnp.logical_or(ki == d0, ki == d1).astype(BF)
    sb[...] = jnp.dot(pack, h_ref[...], preferred_element_type=F32).astype(BF).reshape(sb.shape)
    sends = []
    for k in ORDER:
        off, i = k // 4, k % 4
        c2, t2 = c ^ off, t ^ i
        k2 = c2 * 4 + t2
        if k == 0:
            own = pltpu.make_async_copy(sb.at[me], rb.at[0], dloc.at[0])
            own.start()
        else:
            cp = remote(sb.at[k2], rb.at[k], dsend.at[k], drecv.at[k], c2, t2)
            cp.start()
            sends.append(cp)
    for cp in wl:
        cp.wait()
    for off in (0, 1, 2, 3):
        for i in range(4):
            k = off * 4 + i
            if k == 0:
                own.wait()
            else:
                remote(sb.at[0], rb.at[k], dsend.at[k], drecv.at[k], c ^ off, t ^ i).wait_recv()
        r = rb[off * 4:off * 4 + 4].reshape(4 * cap, -1)
        g = jnp.dot(r, wg[...], preferred_element_type=F32)
        u = jnp.dot(r, wu[...], preferred_element_type=F32)
        a = (g * jax.nn.sigmoid(g) * u).astype(BF)
        z = jnp.dot(a, wd[...], preferred_element_type=F32).astype(BF)
        zb[off * 4:off * 4 + 4] = z.reshape(4, cap, -1)
        for i in range(4):
            k = off * 4 + i
            if k == 0:
                zown = pltpu.make_async_copy(zb.at[0], bb.at[me], zloc.at[0])
                zown.start()
            else:
                cp = remote(zb.at[k], bb.at[me], zsend.at[k], zrecv.at[k], c ^ off, t ^ i)
                cp.start()
                sends.append(cp)
    cols8 = jnp.concatenate([d0, d1, gt, jnp.zeros((4, rows), F32)], axis=0).T
    kj = lax.broadcasted_iota(jnp.int32, (rows, ne * cap), 1).astype(F32)
    s0 = (kj == cols8[:, 0:1]).astype(BF)
    s1 = (kj == cols8[:, 1:2]).astype(BF)
    zown.wait()
    for k in range(1, 16):
        c2, t2 = c ^ (k // 4), t ^ (k % 4)
        remote(zb.at[0], bb.at[c2 * 4 + t2], zsend.at[k], zrecv.at[k], c2, t2).wait_recv()
    for nb in range(4):
        cols = slice(nb * 512, (nb + 1) * 512)
        b = bb[:, :, cols].reshape(ne * cap, 512)
        z0 = jnp.dot(s0, b, preferred_element_type=F32)
        z1 = jnp.dot(s1, b, preferred_element_type=F32)
        out = cols8[:, 2:3] * z0 + cols8[:, 3:4] * z1
        y_ref[:, cols] = (h_ref[:, cols].astype(F32) + out).astype(BF)
    for cp in sends:
        cp.wait_send()


def expert_loads(w1g_ref, w1u_ref, w2_ref, wg, wu, wd, wsem):
    return [pltpu.make_async_copy(a.at[0], b, wsem.at[i])
            for i, (a, b) in enumerate(((w1g_ref, wg), (w1u_ref, wu), (w2_ref, wd)))]


def kernel_c(cap, h_ref, it_ref, gt_ref, w1g_ref, w1u_ref, w2_ref, y_ref, wg, wu, wd, sb, rb, zb, bb, wsem, *sems):
    c = lax.axis_index('cp')
    t = lax.axis_index('tp')
    wl = expert_loads(w1g_ref, w1u_ref, w2_ref, wg, wu, wd, wsem)
    for cp in wl:
        cp.start()
    group_barrier(c, t)
    experts(cap, c, t, h_ref, it_ref[...], gt_ref[...], y_ref, wl, wg, wu, wd, sb, rb, zb, bb, *sems)


def params(cid):
    return pltpu.CompilerParams(collective_id=cid, has_side_effects=True, vmem_limit_bytes=63 * MIB)


def solution(mesh):
    rows_spec = P(('dp', 'cp', 'tp'), None)
    exp_spec = P(('cp', 'tp'), None, None)
    DMA = pltpu.SemaphoreType.DMA

    def local(x, idx, gates, wq, wk, wv, wo, w1g, w1u, w2):
        rows, d = x.shape
        seg = 2 * rows
        hc = wq.shape[1]
        ff = w1g.shape[2]
        sds = jax.ShapeDtypeStruct
        ew = [pltpu.VMEM((d, ff), BF), pltpu.VMEM((d, ff), BF), pltpu.VMEM((ff, d), BF)]
        es = [DMA((16,)), DMA((16,)), DMA((16,)), DMA((16,)), DMA((1,)), DMA((1,))]
        it, gt = idx.T, gates.T
        y, h, over = pl.pallas_call(
            kernel_ab, name='block',
            out_shape=(sds((rows, d), BF), sds((rows, d), BF), sds((1,), jnp.int32)),
            in_specs=[ANY, VM, VM] + [ANY] * 7, out_specs=(VM, ANY, pl.BlockSpec(memory_space=pltpu.SMEM)),
            scratch_shapes=[
                pltpu.VMEM((4 * rows, d), BF), pltpu.VMEM((d, hc), BF), pltpu.VMEM((d, hc), BF), pltpu.VMEM((d, hc), BF),
                pltpu.VMEM((2, 2, 4, seg, HD), BF), pltpu.VMEM((2, 4, HD, seg), BF),
                pltpu.VMEM((2, 2, 8, seg, HD), BF), pltpu.VMEM((2, 8, HD, seg), BF),
                pltpu.VMEM((2, 8, HD, seg), F32), pltpu.VMEM((2, 8, 1, seg), F32), pltpu.VMEM((2, 8, 1, seg), F32),
                pltpu.VMEM((4, hc, d), BF), pltpu.VMEM((2, 8, seg, HD), BF), pltpu.VMEM((rows, d), BF), pltpu.VMEM((rows, d), BF),
                pltpu.VMEM((8, HD), F32), pltpu.VMEM((16, 8, HD), F32)]
            + ew + [pltpu.VMEM((16, BASE_CAP, d), BF)] * 4
            + [DMA((5,)), DMA((3,)), DMA((4,)), DMA((3,)), DMA((4,)), DMA((2, 3, 4, 2)), DMA((2, 3, 8)), DMA((2, 3, 2)),
               DMA((2, 8, 2)), DMA((16,)), DMA((16,)), DMA((16,)), DMA((1,)), DMA((3,))] + es,
            compiler_params=params(0))(x, it, gt, wq, wk, wv, wo, w1g, w1u, w2)

        def full(h, y):
            return pl.pallas_call(
                functools.partial(kernel_c, FULL_CAP), name='experts_full',
                out_shape=sds((rows, d), BF),
                in_specs=[VM, VM, VM, ANY, ANY, ANY], out_specs=VM,
                scratch_shapes=ew + [pltpu.VMEM((16, FULL_CAP, d), BF)] * 4 + [DMA((3,))] + es,
                compiler_params=params(1))(h, it, gt, w1g, w1u, w2)

        return lax.cond(over[0] > 0, full, lambda h, y: y, h, y)

    return jax.shard_map(local, mesh=mesh, in_specs=(rows_spec, rows_spec, rows_spec, P(None, 'tp'), P(None, 'tp'), P(None, 'tp'), P('tp', None), exp_spec, exp_spec, exp_spec), out_specs=rows_spec, check_vma=False)
```

profile of v0, /device:TPU:15, one launch (start us, length us, event | category | flops | bytes accessed | tf_op | source)
XLA Modules:
  0.0 399.3 jit_solution(6551282904183219527)
XLA Ops:
  0.0 0.0 copy-start
  0.0 0.0 copy-start.1
  0.0 195.8 %block.1 = (bf16[256,2048]{1,0:T(8,128)(2,1)}, bf16[256,2048]{1,0:T(8,128)(2,1)}, s32[1]{0:T(128)}) custom-call(bf16[256,2048]{1,0:T(8,128)(2,1)} %x_ref.1, s32[2,256]{1,0:T(2,128)} %bitcast.3, f32[2,256]{1,0:T(2,128)} %bitcast.5, bf16[2048,512]{1,0:T(8,128)(2,1)} %wq_ref.1, bf16[2048,512]{1,0:T(8,128)(2,1)} %wk_ref.1, bf16[2048,512]{1,0:T(8,128)(2,1)} %wv_ref.1, ...), custom_call_target="tpu_custom_call" | custom-call | tf_op jit(solution)/shard_map/block/pallas_call | solution.py:398
  196.4 0.0 copy-done
  196.4 0.0 copy-done.1
  196.4 200.5 %conditional.1 = (bf16[256,2048]{1,0:T(8,128)(2,1)}) conditional(s32[]{:T(128)} %bitcast.2, bf16[256,2048]{1,0:T(8,128)(2,1)} %get-tuple-element.31, (bf16[256,2048]{1,0:T(8,128)(2,1)}, s32[2,256]{1,0:T(2,128)S(1)}, f32[2,256]{1,0:T(2,128)S(1)}, bf16[1,2048,1024]{2,1,0:T(8,128)(2,1)}, bf16[1,2048,1024]{2,1,0:T(8,128)(2,1)}, ...), branch_computations={%region_0.0_spmd, %region_1.0_spmd} | conditional | bytes 8 | solution.py:422
  196.4 200.5 %experts_full.1 = bf16[256,2048]{1,0:T(8,128)(2,1)} custom-call(bf16[256,2048]{1,0:T(8,128)(2,1)} %get-tuple-element.21.h_ref, s32[2,256]{1,0:T(2,128)S(1)} %get-tuple-element.22.it_ref, f32[2,256]{1,0:T(2,128)S(1)} %get-tuple-element.23.gt_ref, bf16[1,2048,1024]{2,1,0:T(8,128)(2,1)} %get-tuple-element.24.w1g_ref, ...), custom_call_target="tpu_custom_call" | custom-call | tf_op jit(solution)/shard_map/cond/branch_1_fun/experts_full/pallas_call | solution.py:415
  397.0 2.3 copy.16
Async XLA Ops:
  0.0 196.4 %copy-start = (s32[256,2]{0,1:T(2,128)S(1)}, s32[256,2]{0,1:T(2,128)}, u32[]{:S(2)}) copy-start(s32[256,2]{0,1:T(2,128)} %param.13) | copy-start | bytes 6148
  0.0 196.4 %copy-start.1 = (f32[256,2]{0,1:T(2,128)S(1)}, f32[256,2]{0,1:T(2,128)}, u32[]{:S(2)}) copy-start(f32[256,2]{0,1:T(2,128)} %param.14) | copy-start | bytes 6148
where the time goes:
time: 400 us; the launch traced here: 399 us
  Pallas kernels  396 us (99%)
    pallas_call x1, Pallas kernels, full(): pl.pallas_call(functools.partial(kernel_c, FULL_CAP), name='experts_full'...  201 us
    pallas_call x1, Pallas kernels, local(): pl.pallas_call(kernel_ab, name='block', out_shape=(sds((rows, d), BF), sd...  196 us

commit v1 on v0

--- a/solution.py
+++ b/solution.py
@@ -25,11 +25,13 @@
         device_id={'cp': c, 'tp': t}, device_id_type=MESH)
 
 
-def group_barrier(c, t):
+def group_barrier(c, t, twin=None):
     sem = pltpu.get_barrier_semaphore()
     for i in range(1, 16):
         pl.semaphore_signal(sem, inc=1, device_id={'cp': c ^ (i // 4), 'tp': t ^ (i % 4)}, device_id_type=MESH)
-    pl.semaphore_wait(sem, 15)
+    if twin is not None:
+        pl.semaphore_signal(sem, inc=1, device_id={'dp': twin}, device_id_type=MESH)
+    pl.semaphore_wait(sem, 15 if twin is None else 16)
 
 
 def kernel_ab(x_ref, it_ref, gt_ref, wq_ref, wk_ref, wv_ref, wo_ref, w1g_ref, w1u_ref, w2_ref,
@@ -46,15 +48,19 @@
     nseg = 8
     me = c * 4 + t
 
+    def pick(cc):
+        return lax.rem(cc, 2)
+
+    def moved(cc, sl):
+        return jnp.logical_and(odd, sl == 1)
+
     def has(cc, sl, s):
         outer = jnp.logical_or(s < 2, s > 5)
-        kvg = jnp.where(cc < 2, outer, jnp.logical_not(outer))
-        moved = jnp.where(cc < 2, s < 2, s >= 2)
-        return jnp.where(jnp.logical_and(odd, sl == 1), moved, kvg)
+        kept = jnp.where(cc < 2, outer, jnp.logical_not(outer))
+        return jnp.where(moved(cc, sl), jnp.where(cc < 2, s < 2, s >= 2), kept)
 
     def sees(cc, sl, s):
-        moved = jnp.where(cc < 2, 1, 7)
-        return s <= jnp.where(jnp.logical_and(odd, sl == 1), moved, jnp.where(cc < 2, 7, 5))
+        return s <= jnp.where(moved(cc, sl), jnp.where(cc < 2, 1, 7), jnp.where(cc < 2, 7, 5))
 
     own = pl.ds(pl.multiple_of(t * rows, rows), rows)
     loads = [pltpu.make_async_copy(a, b, ldsem.at[i])
@@ -64,15 +70,19 @@
     e = lax.broadcasted_iota(jnp.int32, (HD, rows), 0)
     hit = (it_ref[0:1, :] == e).astype(F32) + (it_ref[1:2, :] == e).astype(F32)
     load = jnp.max(jnp.sum(hit, axis=1, keepdims=True), axis=0, keepdims=True)
-    cb[...] = jnp.broadcast_to(load, cb.shape)
-    cnt[me] = cb[...]
-    group_barrier(c, t)
+    cb[0] = jnp.broadcast_to(load, cb.shape[1:])
+    twin = 1 - lax.axis_index('dp')
+    group_barrier(c, t, twin)
     pending = []
 
     def go(cp):
         cp.start()
         pending.append(cp)
 
+    tw = pltpu.make_async_remote_copy(
+        src_ref=cb.at[0], dst_ref=cb.at[1], send_sem=csend.at[0], recv_sem=crecv.at[16],
+        device_id={'dp': twin}, device_id_type=MESH)
+    go(tw)
     loads[0].wait()
     go(remote(xs.at[own], xs.at[own], xsend.at[0], xrecv.at[t], c, t ^ 1))
     go(remote(xs.at[own], xs.at[own], xsend.at[1], xrecv.at[t], c, t ^ 2))
@@ -82,7 +92,7 @@
         remote(xs.at[r], xs.at[r], xsend.at[0], xrecv.at[tt], c, t ^ 1).wait_recv()
 
     def blocks(m, p, cc, sl, s):
-        hd = 2 * sl + lax.rem(cc, 2)
+        hd = 2 * sl + pick(cc)
         if m == 2:
             return sv.at[p, hd], vt.at[sl, s]
         return sqk.at[p, m, hd], qk.at[sl, m, s]
@@ -90,53 +100,68 @@
     def need(m, cc, sl, s):
         return has(cc, sl, s) if m == 0 else sees(cc, sl, s)
 
-    def block_copy(m, p, off, sl, s):
+    core = lax.rem(t, 2)
+
+    def cut(m, ref, part):
+        at = pl.ds(pl.multiple_of((core ^ part) * rows, rows), rows)
+        return ref.at[:, at] if m == 2 else ref.at[at]
+
+    def block_copy(m, p, off, sl, s, part):
         cc = c ^ off
         src, dst = blocks(m, p, cc, sl, s)
-        return need(m, cc, sl, s), remote(src, dst, bsend.at[p, m, off, sl], brecv.at[sl, m, s], cc, t)
+        return need(m, cc, sl, s), remote(cut(m, src, part), cut(m, dst, part), bsend.at[p, m, off, 2 * sl + part], brecv.at[sl, m, s], cc, t)
 
     def own_copy(m, p, sl, s):
         src, dst = blocks(m, p, c, sl, s)
         return need(m, c, sl, s), pltpu.make_async_copy(src, dst, bloc.at[p, m, sl])
 
-    def half(p, row0, s):
+    def half(p, tt, s, arrive):
         for sl in range(2):
             wide = slice(2 * sl * HD, 2 * (sl + 1) * HD)
-            for m, w, ld in ((1, wk, 1), (2, wv, 2), (0, wq, 3)):
-                if p == 0 and sl == 0:
-                    loads[ld].wait()
-                r = jnp.dot(xs[pl.ds(row0, seg), :], w[:, wide], preferred_element_type=F32)
-                if m == 2:
-                    rt = r.T.astype(BF)
-                    for hh in range(2):
-                        sv[p, 2 * sl + hh] = rt[hh * HD:(hh + 1) * HD]
-                else:
-                    r = r.astype(BF)
-                    for hh in range(2):
-                        sqk[p, m, 2 * sl + hh] = r[:, hh * HD:(hh + 1) * HD]
-                for off in (1, 2, 3):
-                    ok, cp = block_copy(m, p, off, sl, s)
-                    pl.when(ok)(cp.start)
+            for part in range(2):
+                if sl == 0:
+                    arrive[part]()
+                at = pl.ds(pl.multiple_of((core ^ part) * rows, rows), rows)
+                xp = xs[pl.ds(pl.multiple_of((tt ^ part) * rows, rows), rows), :]
+                for m, w, ld in ((1, wk, 1), (2, wv, 2), (0, wq, 3)):
+                    if p == 0 and sl == 0 and part == 0:
+                        loads[ld].wait()
+                    r = jnp.dot(xp, w[:, wide], preferred_element_type=F32)
+                    if m == 2:
+                        rt = r.T.astype(BF)
+                        for hh in range(2):
+                            sv[p, 2 * sl + hh, :, at] = rt[hh * HD:(hh + 1) * HD]
+                    else:
+                        r = r.astype(BF)
+                        for hh in range(2):
+                            sqk[p, m, 2 * sl + hh, at] = r[:, hh * HD:(hh + 1) * HD]
+                    for off in (1, 2, 3):
+                        ok, cp = block_copy(m, p, off, sl, s, part)
+                        pl.when(ok)(cp.start)
+            for m in range(3):
                 ok, cp = own_copy(m, p, sl, s)
                 pl.when(ok)(cp.start)
 
     seg0 = jnp.where(y == 0, c, nseg - 1 - c)
     seg1 = jnp.where(y == 0, nseg - 1 - c, c)
-    xwait(t ^ 1)
-    half(0, pl.multiple_of(y * seg, seg), seg0)
+    half(0, t, seg0, (lambda: None, lambda: xwait(t ^ 1)))
     loads[4].wait()
     go(remote(wob.at[t], wob.at[t], wsend.at[0], wrecv.at[t], c, t ^ 1))
     go(remote(wob.at[t], wob.at[t], wsend.at[1], wrecv.at[t], c, t ^ 2))
+    tw.wait_recv()
+    cb[2] = jnp.maximum(cb[0], cb[1])
+    cnt[me] = cb[2]
     for i in range(1, 16):
-        go(remote(cb, cnt.at[me], csend.at[i], crecv.at[me], c ^ (i // 4), t ^ (i % 4)))
+        go(remote(cb.at[2], cnt.at[me], csend.at[i], crecv.at[me], c ^ (i // 4), t ^ (i % 4)))
     acc[...] = jnp.zeros_like(acc)
     mx[...] = jnp.full_like(mx, NEG)
     ls[...] = jnp.zeros_like(ls)
-    xwait(t ^ 2)
-    r2 = pl.ds(pl.multiple_of((t ^ 2) * rows, rows), rows)
-    go(remote(xs.at[r2], xs.at[r2], xsend.at[2], xrecv.at[t ^ 2], c, t ^ 1))
-    xwait(t ^ 3)
-    half(1, pl.multiple_of((1 - y) * seg, seg), seg1)
+    def pass_on():
+        xwait(t ^ 2)
+        r2 = pl.ds(pl.multiple_of((t ^ 2) * rows, rows), rows)
+        go(remote(xs.at[r2], xs.at[r2], xsend.at[2], xrecv.at[t ^ 2], c, t ^ 1))
+
+    half(1, t ^ 2, seg1, (pass_on, lambda: xwait(t ^ 3)))
     wl = expert_loads(w1g_ref, w1u_ref, w2_ref, wg, wu, wd, esem)
     for cp in wl:
         cp.start()
@@ -181,7 +206,7 @@
 
     def ocopy(sl, s, hf):
         c2, t2 = dest(s, hf)
-        hd = t * 4 + 2 * sl + lax.rem(c, 2)
+        hd = t * 4 + 2 * sl + pick(c)
         src = ob.at[sl, s, pl.ds(hf * rows, rows)]
         dst = orecv.at[:, pl.ds(pl.multiple_of(hd * HD, HD), HD)]
         rm = remote(src, dst, osend.at[sl, s, hf], orsem.at[hd], c2, t2)
@@ -244,16 +269,16 @@
     go(remote(wob.at[t ^ 2], wob.at[t ^ 2], wsend.at[2], wrecv.at[t ^ 2], c, t ^ 1))
     for i in range(1, 16):
         other = (c ^ (i // 4)) * 4 + (t ^ (i % 4))
-        remote(cb, cnt.at[other], csend.at[i], crecv.at[other], c ^ (i // 4), t ^ (i % 4)).wait_recv()
+        remote(cb.at[2], cnt.at[other], csend.at[i], crecv.at[other], c ^ (i // 4), t ^ (i % 4)).wait_recv()
     worst = jnp.max(cnt[...])
     over_ref[0] = (worst > BASE_CAP).astype(jnp.int32)
     for tt in range(4):
         for hd in range(4):
             k = tt * 4 + hd
             half_b = jnp.logical_and(seg0 >= 2, seg0 <= 5)
-            if hd >= 2 and tt % 2 == 1:
+            if tt % 2 == 1 and hd >= 2:
                 half_b = seg0 >= 2
-            cp_ = jnp.where(half_b, 2, 0) + hd % 2
+            cp_ = jnp.where(half_b, 2 + hd % 2, hd % 2)
             mine = jnp.logical_and(cp_ == c, t == tt)
             dst = orecv.at[:, k * HD:(k + 1) * HD]
             src = ob.at[0, 0, pl.ds(0, rows)]
@@ -278,8 +303,9 @@
         for m in range(3):
             for off in (1, 2, 3):
                 for sl in range(2):
-                    ok, cp = block_copy(m, p, off, sl, s)
-                    pl.when(ok)(cp.wait_send)
+                    for part in range(2):
+                        ok, cp = block_copy(m, p, off, sl, s, part)
+                        pl.when(ok)(cp.wait_send)
 
     def drain(s, _):
         for sl in range(2):
@@ -321,28 +347,35 @@
             sends.append(cp)
     for cp in wl:
         cp.wait()
-    for off in (0, 1, 2, 3):
+    zown = pltpu.make_async_copy(zb.at[0], bb.at[me], zloc.at[0])
+
+    def back(k):
+        return remote(zb.at[k], bb.at[me], zsend.at[k], zrecv.at[k], c ^ (k // 4), t ^ lax.rem(k, 4))
+
+    def group(off, _):
         for i in range(4):
             k = off * 4 + i
-            if k == 0:
-                own.wait()
+            arrived = remote(sb.at[0], rb.at[k], dsend.at[k], drecv.at[k], c ^ off, t ^ i).wait_recv
+            if i == 0:
+                pl.when(off == 0)(own.wait)
+                pl.when(off > 0)(arrived)
             else:
-                remote(sb.at[0], rb.at[k], dsend.at[k], drecv.at[k], c ^ off, t ^ i).wait_recv()
-        r = rb[off * 4:off * 4 + 4].reshape(4 * cap, -1)
+                arrived()
+        r = rb[pl.ds(off * 4, 4)].reshape(4 * cap, -1)
         g = jnp.dot(r, wg[...], preferred_element_type=F32)
         u = jnp.dot(r, wu[...], preferred_element_type=F32)
         a = (g * jax.nn.sigmoid(g) * u).astype(BF)
         z = jnp.dot(a, wd[...], preferred_element_type=F32).astype(BF)
-        zb[off * 4:off * 4 + 4] = z.reshape(4, cap, -1)
+        zb[pl.ds(off * 4, 4)] = z.reshape(4, cap, -1)
         for i in range(4):
-            k = off * 4 + i
-            if k == 0:
-                zown = pltpu.make_async_copy(zb.at[0], bb.at[me], zloc.at[0])
-                zown.start()
+            if i == 0:
+                pl.when(off == 0)(zown.start)
+                pl.when(off > 0)(back(off * 4).start)
             else:
-                cp = remote(zb.at[k], bb.at[me], zsend.at[k], zrecv.at[k], c ^ off, t ^ i)
-                cp.start()
-                sends.append(cp)
+                back(off * 4 + i).start()
+        return 0
+
+    lax.fori_loop(0, 4, group, 0)
     cols8 = jnp.concatenate([d0, d1, gt, jnp.zeros((4, rows), F32)], axis=0).T
     kj = lax.broadcasted_iota(jnp.int32, (rows, ne * cap), 1).astype(F32)
     s0 = (kj == cols8[:, 0:1]).astype(BF)
@@ -360,6 +393,8 @@
         y_ref[:, cols] = (h_ref[:, cols].astype(F32) + out).astype(BF)
     for cp in sends:
         cp.wait_send()
+    for k in range(1, 16):
+        back(k).wait_send()
 
 
 def expert_loads(w1g_ref, w1u_ref, w2_ref, wg, wu, wd, wsem):
@@ -378,7 +413,7 @@
 
 
 def params(cid):
-    return pltpu.CompilerParams(collective_id=cid, has_side_effects=True, vmem_limit_bytes=63 * MIB)
+    return pltpu.CompilerParams(collective_id=cid, has_side_effects=True, vmem_limit_bytes=60 * MIB)
 
 
 def solution(mesh):
@@ -405,10 +440,10 @@
                 pltpu.VMEM((2, 2, 8, seg, HD), BF), pltpu.VMEM((2, 8, HD, seg), BF),
                 pltpu.VMEM((2, 8, HD, seg), F32), pltpu.VMEM((2, 8, 1, seg), F32), pltpu.VMEM((2, 8, 1, seg), F32),
                 pltpu.VMEM((4, hc, d), BF), pltpu.VMEM((2, 8, seg, HD), BF), pltpu.VMEM((rows, d), BF), pltpu.VMEM((rows, d), BF),
-                pltpu.VMEM((8, HD), F32), pltpu.VMEM((16, 8, HD), F32)]
+                pltpu.VMEM((3, 8, HD), F32), pltpu.VMEM((16, 8, HD), F32)]
             + ew + [pltpu.VMEM((16, BASE_CAP, d), BF)] * 4
-            + [DMA((5,)), DMA((3,)), DMA((4,)), DMA((3,)), DMA((4,)), DMA((2, 3, 4, 2)), DMA((2, 3, 8)), DMA((2, 3, 2)),
-               DMA((2, 8, 2)), DMA((16,)), DMA((16,)), DMA((16,)), DMA((1,)), DMA((3,))] + es,
+            + [DMA((5,)), DMA((3,)), DMA((4,)), DMA((3,)), DMA((4,)), DMA((2, 3, 4, 4)), DMA((2, 3, 8)), DMA((2, 3, 2)),
+               DMA((2, 8, 2)), DMA((16,)), DMA((16,)), DMA((17,)), DMA((1,)), DMA((3,))] + es,
             compiler_params=params(0))(x, it, gt, wq, wk, wv, wo, w1g, w1u, w2)
 
         def full(h, y):

time: 400 us -> 395 us (0.988)
  Pallas kernels: 396 us -> 392 us
where the time goes in v1:
time: 395 us; the launch traced here: 393 us
  Pallas kernels  392 us (99%)
    pallas_call x1, Pallas kernels, full(): pl.pallas_call(functools.partial(kernel_c, FULL_CAP), name='experts_full'...  198 us
    pallas_call x1, Pallas kernels, local(): pl.pallas_call(kernel_ab, name='block', out_shape=(sds((rows, d), BF), sd...  193 us

profile of v1, /device:TPU:15, one launch (start us, length us, event | category | flops | bytes accessed | tf_op | source)
XLA Modules:
  0.0 393.4 jit_solution(7517893916976542728)
XLA Ops:
  0.0 0.0 copy-start
  0.0 0.0 copy-start.1
  0.0 193.4 %block.1 = (bf16[256,2048]{1,0:T(8,128)(2,1)S(1)}, bf16[256,2048]{1,0:T(8,128)(2,1)S(1)}, s32[1]{0:T(128)}) custom-call(bf16[256,2048]{1,0:T(8,128)(2,1)} %x_ref.1, s32[2,256]{1,0:T(2,128)} %bitcast.3, f32[2,256]{1,0:T(2,128)} %bitcast.5, bf16[2048,512]{1,0:T(8,128)(2,1)} %wq_ref.1, bf16[2048,512]{1,0:T(8,128)(2,1)} %wk_ref.1, bf16[2048,512]{1,0:T(8,128)(2,1)} %wv_ref.1, ...), custom_call_target="tpu_custom_call" | custom-call | tf_op jit(solution)/shard_map/block/pallas_call | solution.py:433
  194.0 0.0 copy-done
  194.0 0.0 copy-done.1
  194.1 198.4 %conditional.1 = (bf16[256,2048]{1,0:T(8,128)(2,1)S(1)}) conditional(s32[]{:T(128)} %bitcast.2, bf16[256,2048]{1,0:T(8,128)(2,1)S(1)} %get-tuple-element.31, (bf16[256,2048]{1,0:T(8,128)(2,1)S(1)}, s32[2,256]{1,0:T(2,128)S(1)}, f32[2,256]{1,0:T(2,128)S(1)}, bf16[1,2048,1024]{2,1,0:T(8,128)(2,1)}, bf16[1,2048,1024]{2,1,0:T(8,128)(2,1)}, ...), branch_computations={%region_0.0_spmd, %region_1.0_spmd} | conditional | bytes 8 | solution.py:457
  194.3 198.1 %experts_full.1 = bf16[256,2048]{1,0:T(8,128)(2,1)S(1)} custom-call(bf16[256,2048]{1,0:T(8,128)(2,1)S(1)} %get-tuple-element.21.h_ref, s32[2,256]{1,0:T(2,128)S(1)} %get-tuple-element.22.it_ref, f32[2,256]{1,0:T(2,128)S(1)} %get-tuple-element.23.gt_ref, bf16[1,2048,1024]{2,1,0:T(8,128)(2,1)} %get-tuple-element.24.w1g_ref, ...), custom_call_target="tpu_custom_call" | custom-call | tf_op jit(solution)/shard_map/cond/branch_1_fun/experts_full/pallas_call | solution.py:450
  392.4 1.0 copy.16
Async XLA Ops:
  0.0 194.0 %copy-start = (s32[256,2]{0,1:T(2,128)S(1)}, s32[256,2]{0,1:T(2,128)}, u32[]{:S(2)}) copy-start(s32[256,2]{0,1:T(2,128)} %param.13) | copy-start | bytes 6148
  0.0 194.0 %copy-start.1 = (f32[256,2]{0,1:T(2,128)S(1)}, f32[256,2]{0,1:T(2,128)}, u32[]{:S(2)}) copy-start(f32[256,2]{0,1:T(2,128)} %param.14) | copy-start | bytes 6148

commit v2 on v1

--- a/solution.py
+++ b/solution.py
@@ -220,7 +220,17 @@
             pl.when(jnp.logical_not(mine))(rm.start)
             pl.when(mine)(lc.start)
 
+    def wwait(tt):
+        remote(wob.at[t], wob.at[tt], wsend.at[0], wrecv.at[tt], c, t ^ 1).wait_recv()
+
+    wpass = remote(wob.at[t ^ 2], wob.at[t ^ 2], wsend.at[2], wrecv.at[t ^ 2], c, t ^ 1)
+
     def event(ev, _):
+        @pl.when(ev == 15)
+        def _():
+            wwait(t ^ 2)
+            wpass.start()
+
         p = ev // 8
         sl = lax.rem(ev // 4, 2)
         i = p * 4 + lax.rem(ev, 4)
@@ -261,38 +271,43 @@
         return 0
 
     lax.fori_loop(0, 16, event, 0)
-
-    def wwait(tt):
-        remote(wob.at[t], wob.at[tt], wsend.at[0], wrecv.at[tt], c, t ^ 1).wait_recv()
-
-    wwait(t ^ 2)
-    go(remote(wob.at[t ^ 2], wob.at[t ^ 2], wsend.at[2], wrecv.at[t ^ 2], c, t ^ 1))
+    pending.append(wpass)
+
     for i in range(1, 16):
         other = (c ^ (i // 4)) * 4 + (t ^ (i % 4))
         remote(cb.at[2], cnt.at[other], csend.at[i], crecv.at[other], c ^ (i // 4), t ^ (i % 4)).wait_recv()
     worst = jnp.max(cnt[...])
     over_ref[0] = (worst > BASE_CAP).astype(jnp.int32)
-    for tt in range(4):
-        for hd in range(4):
-            k = tt * 4 + hd
-            half_b = jnp.logical_and(seg0 >= 2, seg0 <= 5)
-            if tt % 2 == 1 and hd >= 2:
-                half_b = seg0 >= 2
-            cp_ = jnp.where(half_b, 2 + hd % 2, hd % 2)
-            mine = jnp.logical_and(cp_ == c, t == tt)
-            dst = orecv.at[:, k * HD:(k + 1) * HD]
-            src = ob.at[0, 0, pl.ds(0, rows)]
-            pl.when(jnp.logical_not(mine))(remote(src, dst, osend.at[0, 0, 0], orsem.at[k], c, t ^ 1).wait_recv)
-            pl.when(mine)(pltpu.make_async_copy(src, dst, orsem.at[k]).wait)
+    def owait(tt, hd):
+        k = tt * 4 + hd
+        half_b = jnp.logical_and(seg0 >= 2, seg0 <= 5)
+        if tt % 2 == 1 and hd >= 2:
+            half_b = seg0 >= 2
+        cp_ = jnp.where(half_b, 2 + hd % 2, hd % 2)
+        mine = jnp.logical_and(cp_ == c, t == tt)
+        dst = orecv.at[:, k * HD:(k + 1) * HD]
+        src = ob.at[0, 0, pl.ds(0, rows)]
+        pl.when(jnp.logical_not(mine))(remote(src, dst, osend.at[0, 0, 0], orsem.at[k], c, t ^ 1).wait_recv)
+        pl.when(mine)(pltpu.make_async_copy(src, dst, orsem.at[k]).wait)
+
     wwait(t ^ 1)
     wwait(t ^ 3)
-    for nb in range(4):
-        cols = slice(nb * 512, (nb + 1) * 512)
-        a = xs[own, cols].astype(F32)
-        p = jnp.zeros_like(a)
+    for sl in range(2):
         for tt in range(4):
-            p = p + jnp.dot(orecv[:, tt * 512:(tt + 1) * 512], wob[tt, :, cols], preferred_element_type=F32)
-        hs[:, cols] = (a + p).astype(BF)
+            for hd in (2 * sl, 2 * sl + 1):
+                owait(tt, hd)
+        ks = slice(2 * sl * HD, 2 * (sl + 1) * HD)
+        for nb in range(4):
+            cols = slice(nb * 512, (nb + 1) * 512)
+            p = xs[own, cols].astype(F32) if sl else jnp.zeros((rows, 512), F32)
+            q = acc[0, 2 * nb:2 * nb + 2].reshape(rows, 512) if sl else jnp.zeros((rows, 512), F32)
+            for tt in range(4):
+                o = orecv[:, tt * 512 + 2 * sl * HD:tt * 512 + 2 * (sl + 1) * HD]
+                q = q + jnp.dot(o, wob[tt, ks, cols], preferred_element_type=F32)
+            if sl:
+                hs[:, cols] = (p + q).astype(BF)
+            else:
+                acc[0, 2 * nb:2 * nb + 2] = q.reshape(2, HD, 512)
     hcp = pltpu.make_async_copy(hs, h_out, hsem.at[0])
     hcp.start()
     experts(BASE_CAP, c, t, hs, it_ref[...], gt_ref[...], y_ref, wl, wg, wu, wd, sb, rb, zb, bb, *csems)

time: 395 us -> 394 us (level)
  no operation moved by 1% of the time
where the time goes in v2:
time: 394 us; the launch traced here: 392 us
  Pallas kernels  391 us (99%)
    pallas_call x1, Pallas kernels, full(): pl.pallas_call(functools.partial(kernel_c, FULL_CAP), name='experts_full'...  198 us
    pallas_call x1, Pallas kernels, local(): pl.pallas_call(kernel_ab, name='block', out_shape=(sds((rows, d), BF), sd...  192 us

profile of v2, /device:TPU:15, one launch (start us, length us, event | category | flops | bytes accessed | tf_op | source)
XLA Modules:
  0.0 392.5 jit_solution(14156895460143578305)
XLA Ops:
  0.0 0.0 copy-start
  0.0 0.0 copy-start.1
  0.0 192.3 %block.1 = (bf16[256,2048]{1,0:T(8,128)(2,1)S(1)}, bf16[256,2048]{1,0:T(8,128)(2,1)S(1)}, s32[1]{0:T(128)}) custom-call(bf16[256,2048]{1,0:T(8,128)(2,1)} %x_ref.1, s32[2,256]{1,0:T(2,128)} %bitcast.3, f32[2,256]{1,0:T(2,128)} %bitcast.5, bf16[2048,512]{1,0:T(8,128)(2,1)} %wq_ref.1, bf16[2048,512]{1,0:T(8,128)(2,1)} %wk_ref.1, bf16[2048,512]{1,0:T(8,128)(2,1)} %wv_ref.1, ...), custom_call_target="tpu_custom_call" | custom-call | tf_op jit(solution)/shard_map/block/pallas_call | solution.py:448
  192.9 0.0 copy-done
  193.0 0.0 copy-done.1
  193.0 198.5 %conditional.1 = (bf16[256,2048]{1,0:T(8,128)(2,1)S(1)}) conditional(s32[]{:T(128)} %bitcast.2, bf16[256,2048]{1,0:T(8,128)(2,1)S(1)} %get-tuple-element.31, (bf16[256,2048]{1,0:T(8,128)(2,1)S(1)}, s32[2,256]{1,0:T(2,128)S(1)}, f32[2,256]{1,0:T(2,128)S(1)}, bf16[1,2048,1024]{2,1,0:T(8,128)(2,1)}, bf16[1,2048,1024]{2,1,0:T(8,128)(2,1)}, ...), branch_computations={%region_0.0_spmd, %region_1.0_spmd} | conditional | bytes 8 | solution.py:472
  193.2 198.3 %experts_full.1 = bf16[256,2048]{1,0:T(8,128)(2,1)S(1)} custom-call(bf16[256,2048]{1,0:T(8,128)(2,1)S(1)} %get-tuple-element.21.h_ref, s32[2,256]{1,0:T(2,128)S(1)} %get-tuple-element.22.it_ref, f32[2,256]{1,0:T(2,128)S(1)} %get-tuple-element.23.gt_ref, bf16[1,2048,1024]{2,1,0:T(8,128)(2,1)} %get-tuple-element.24.w1g_ref, ...), custom_call_target="tpu_custom_call" | custom-call | tf_op jit(solution)/shard_map/cond/branch_1_fun/experts_full/pallas_call | solution.py:465
  391.5 1.0 copy.16
Async XLA Ops:
  0.0 192.9 %copy-start = (s32[256,2]{0,1:T(2,128)S(1)}, s32[256,2]{0,1:T(2,128)}, u32[]{:S(2)}) copy-start(s32[256,2]{0,1:T(2,128)} %param.13) | copy-start | bytes 6148
  0.0 193.0 %copy-start.1 = (f32[256,2]{0,1:T(2,128)S(1)}, f32[256,2]{0,1:T(2,128)}, u32[]{:S(2)}) copy-start(f32[256,2]{0,1:T(2,128)} %param.14) | copy-start | bytes 6148
